TPU v7x, 32 devices: a whole 2x2x4 slice. The times are simulated.
32 devices in a mesh: leaf: 8 (over z, y), probe: 4 (over x, core).
Axes of the slice: x: 2, y: 2, z: 4, core: 2. Of those that a mesh axis runs over, the one named last changes fastest.
Arguments:
- coords: float32 [3, 32768], P(None, 'leaf')
- site_order: int32 [128, 256], P('leaf'), may hold values from 0 to 255, each once within a row
- leaf_pairs: int32 [2, 768], P(None, 'leaf'), may hold values from 0 to 127, as said below
- pair_count: int32 [8], P('leaf'), may hold values from 31 to 96, as said below
- probes: float32 [64, 32768], P('probe', 'leaf'), may hold values from -16 to 16
Outputs:
- solution: float32 [64, 32768], P('probe', 'leaf')
- residual: float32 [64, 32768], P('probe', 'leaf')
Inputs may be any that keep to these rules, and one draw needn't show every extreme that they name: `leaf_pairs`: each leaf index owns 96 slots; its first pair_count slots hold distinct pairs (i, j) with i among that index's own 16 leaves and i <= j <= i + 5, j < 128, every own leaf listed with itself once and with the next leaf where there is one; the later slots hold the index's first leaf twice. `pair_count`: pairs listed for each leaf index; some index lists 96 in every draw. Each row of site_order lists 0 to 255 once.
All inputs are finite; a program needn't handle non-finite values.
Results may differ from a plain program's by a relative error of at most 0.0003.
Values sent between devices are 32-bit elements; how exact they have to be, the bound alone decides.
A program may use at most 64 MiB of HBM per device.

v0:
```python
import math

import jax
import jax.numpy as jnp
from jax import lax
from jax.sharding import PartitionSpec as P

REACH = 5
ITERS = 2


UNIT = 0.025
LENGTH = 0.12
NUGGET = 0.5
UPPER_LIMIT = lax.Precision.HIGHEST


def from_behind(value, axis, by):
    length = lax.axis_size(axis)
    pairs = [(i, i + by) for i in range(length) if 0 <= i + by < length]
    return lax.ppermute(value, axis, pairs)


def kernel_tiles(left, right):
    diff = left[:, :, :, None] - right[:, :, None, :]
    dist = jnp.sqrt(jnp.sum(diff * diff, axis=0))
    taper = REACH * UNIT
    scaled = dist * (math.sqrt(3.0) / LENGTH)
    remain = jnp.maximum(1.0 - dist / taper, 0.0)
    return (1.0 + scaled) * jnp.exp(-scaled) * remain**4 * (1.0 + 4.0 * dist / taper)


def body(coords, site_order, leaf_pairs, pair_count, probes):
    leaf_dev, width = site_order.shape
    columns = probes.shape[0]
    points = jnp.take_along_axis(coords.reshape(3, leaf_dev, width), site_order[None], axis=2)
    next_points = from_behind(points[:, :REACH], "leaf", -1)
    all_points = jnp.concatenate([points, next_points], axis=1)
    base = lax.axis_index("leaf") * leaf_dev
    local_rows = leaf_pairs[0] - base
    leaf_local_columns = leaf_pairs[1] - base
    count = pair_count[0]
    extent = leaf_dev + REACH
    span = 8
    blocks = (count + span - 1) // span
    spots = jnp.arange(extent)
    right = probes.reshape(columns, leaf_dev, width)
    solution = jnp.zeros_like(right)
    residual = right
    direction = right
    norm_now = lax.psum(jnp.sum(residual * residual, axis=(1, 2)), "leaf")
    for step in range(ITERS):
        rim = from_behind(direction[:, :REACH], "leaf", -1)
        whole = lax.all_gather(direction, "probe", axis=0, tiled=True)
        far = lax.all_gather(rim, "probe", axis=0, tiled=True)
        values = jnp.concatenate([whole, far], axis=1)
        first = lax.axis_index("probe")

        def one_block(turn, grand_total):
            start = (first + turn * lax.axis_size("probe")) * span
            rows = lax.dynamic_slice_in_dim(local_rows, start, span)
            cols = lax.dynamic_slice_in_dim(leaf_local_columns, start, span)
            live = (start + jnp.arange(span) < count).astype(jnp.float32)
            tiles = kernel_tiles(
                jnp.take(all_points, rows, axis=1), jnp.take(all_points, cols, axis=1)
            )
            tiles = tiles * live[:, None, None]
            to_row = jnp.einsum(
                "bak,cbk->cba", tiles, jnp.take(values, cols, axis=1), precision=UPPER_LIMIT
            )
            apart = (rows != cols).astype(jnp.float32)
            column_target = jnp.einsum(
                "bak,cba->cbk", tiles, jnp.take(values, rows, axis=1), precision=UPPER_LIMIT
            )
            column_target = column_target * apart[None, :, None]
            row_onehot = (rows[:, None] == spots[None, :]).astype(jnp.float32)
            column_onehot = (cols[:, None] == spots[None, :]).astype(jnp.float32)
            grand_total = grand_total + jnp.einsum(
                "cba,bl->cla", to_row, row_onehot, precision=UPPER_LIMIT
            )
            return grand_total + jnp.einsum(
                "egs,gu->eus", column_target, column_onehot, precision=UPPER_LIMIT
            )

        turns = (blocks - first + lax.axis_size("probe") - 1) // lax.axis_size("probe")
        summed = lax.fori_loop(0, turns, one_block, jnp.zeros(values.shape, jnp.float32))
        reduced = lax.psum_scatter(summed, "probe", scatter_dimension=0, tiled=True)
        operator_back = from_behind(reduced[:, leaf_dev:], "leaf", 1)
        front = reduced[:, :leaf_dev]
        own = jnp.concatenate([front[:, :REACH] + operator_back, front[:, REACH:]], axis=1)
        image = NUGGET * direction + own
        curve = lax.psum(jnp.sum(direction * image, axis=(1, 2)), "leaf")
        alpha = norm_now / curve
        solution = solution + alpha[:, None, None] * direction
        residual = residual - alpha[:, None, None] * image
        if step + 1 < ITERS:
            norm_next = lax.psum(jnp.sum(residual * residual, axis=(1, 2)), "leaf")
            direction = residual + (norm_next / norm_now)[:, None, None] * direction
            norm_now = norm_next
    return (
        solution.reshape(columns, leaf_dev * width),
        residual.reshape(columns, leaf_dev * width),
    )


def solution(mesh):
    in_specs = (P(None, "leaf"), P("leaf", None), P(None, "leaf"), P("leaf"), P("probe", "leaf"))
    out_specs = (P("probe", "leaf"), P("probe", "leaf"))
    return jax.shard_map(body, mesh=mesh, in_specs=in_specs, out_specs=out_specs, check_vma=False)
```

profile of v0, /device:TPU:0, one launch (start us, length us, event | category | flops | bytes accessed | tf_op | source)
XLA Modules:
  0.0 370.1 jit_solution(553922527414436100)
XLA Ops:
  12.8 44.6 %gather_fusion.8 = f32[4096,3]{1,0:T(8,128)} fusion(f32[3,16,256]{0,2,1:T(8,128)S(1)} %bitcast.125, s32[4096]{0:T(1024)S(1)} %bitcast.117), kind=kCustom, calls=%fused_computation.8 | custom fusion | bytes 131072 | tf_op jit(solution)/shard_map/jit(take_along_axis)/gather | solution.py:36
  61.7 5.3 %collective-permute-done.1 = f32[3,5,256]{2,0,1:T(4,128)S(1)} collective-permute-done((f32[3,5,256]{2,0,1:T(4,128)S(1)}, f32[3,5,256]{2,0,1:T(4,128)S(1)}, u32[]{:S(2)}, u32[]{:S(2)}) %collective-permute-start.1) | collective-permute-done | bytes 15392 | tf_op jit(solution)/shard_map/ppermute | solution.py:21
  67.0 6.6 %all_gather.13 = f32[64,5,256]{2,0,1:T(8,128)S(1)} all-gather(f32[16,5,256]{2,0,1:T(8,128)S(1)} %copy.53), channel_id=1, replica_groups=mesh['leaf'=8,'probe'=4] {'probe'}, dimensions={0}, use_global_device_ids=true | all-gather | bytes 409600 | tf_op jit(solution)/shard_map/all_gather | solution.py:55
  76.9 43.9 %while.28 = (s32[]{:T(128)}, f32[64,21,256]{2,1,0:T(8,128)S(1)}, s32[]{:T(128)}, s32[]{:T(128)}, s32[96]{0:T(128)S(1)}, /*index=5*/s32[96]{0:T(128)S(1)}, f32[64...) while((s32[]{:T(128)}, f32[64,21,256]{2,1,0:T(8,128)S(1)}, ...), condition=%wide.region_4.7_spmd.clone.clone, body=%wide.region_2.0_spmd.clone.clone.sunk | while | flops 891337280 | bytes 17392616 | solution.py:86
  83.6 5.1 %convolution_bitcast_fusion.4 = f32[64,8,256]{2,0,1:T(8,128)S(1)} fusion(f32[8,64,256]{2,1,0:T(8,128)S(1)} %gather_fusion, pred[8]{0:T(512)(128)(4,1)S(1)} %compare_and_fusion.9, f32[8,256,256]{2,1,0:T(8,128)} %multiply_reduce_fusion.8, f32[8]{0:T(128)S(1)} %get-tuple-element.579), kind=kOutput, calls=%fused_computation.15.clone.1 | convolution fusion | flops 410124288 | bytes 3145768 | tf_op jit(solution)/shard_map/while/body/bak,cbk->cba/dot_general | solution.py:68
  89.8 2.7 gather_fusion.3
  92.5 4.7 %fusion.68 = f32[64,8,256]{2,0,1:T(8,128)S(1)} fusion(f32[8,64,256]{2,1,0:T(8,128)} %gather_fusion.3, f32[8]{0:T(128)S(1)} %get-tuple-element.580, pred[8]{0:T(512)(128)(4,1)S(1)} %compare_and_fusion.10, f32[8,256,256]{2,1,0:T(8,128)} %multiply_reduce_fusion.8, f32[8]{0:T(128)S(1)} %get-tuple-element.579), kind=kOutput, calls=%fused_computation.17.clone.1 | convolution fusion | flops 410255360 | bytes 3145800 | tf_op jit(solution)/shard_map/while/body/bak,cba->cbk/dot_general | solution.py:72
  105.5 5.1 %convolution_bitcast_fusion.4 = f32[64,8,256]{2,0,1:T(8,128)S(1)} fusion(f32[8,64,256]{2,1,0:T(8,128)S(1)} %gather_fusion, pred[8]{0:T(512)(128)(4,1)S(1)} %compare_and_fusion.9, f32[8,256,256]{2,1,0:T(8,128)} %multiply_reduce_fusion.8, f32[8]{0:T(128)S(1)} %get-tuple-element.579), kind=kOutput, calls=%fused_computation.15.clone.1 | convolution fusion | flops 410124288 | bytes 3145768 | tf_op jit(solution)/shard_map/while/body/bak,cbk->cba/dot_general | solution.py:68
  111.6 2.7 gather_fusion.3
  114.3 4.7 %fusion.68 = f32[64,8,256]{2,0,1:T(8,128)S(1)} fusion(f32[8,64,256]{2,1,0:T(8,128)} %gather_fusion.3, f32[8]{0:T(128)S(1)} %get-tuple-element.580, pred[8]{0:T(512)(128)(4,1)S(1)} %compare_and_fusion.10, f32[8,256,256]{2,1,0:T(8,128)} %multiply_reduce_fusion.8, f32[8]{0:T(128)S(1)} %get-tuple-element.579), kind=kOutput, calls=%fused_computation.17.clone.1 | convolution fusion | flops 410255360 | bytes 3145800 | tf_op jit(solution)/shard_map/while/body/bak,cba->cbk/dot_general | solution.py:72
  122.1 49.5 %reduce-scatter.3.cloned.1.call-done = f32[16,21,256]{2,1,0:T(8,128)} async-done(((f32[64,21,256]{2,1,0:T(8,128)}), f32[16,21,256]{2,1,0:T(8,128)}) %reduce-scatter.3.cloned.1.call-update) | async-done | bytes 344080 | tf_op jit(solution)/shard_map/reduce_scatter | solution.py:87
  172.4 3.4 collective-permute-start.2
  179.7 22.4 %all-reduce = (f32[16]{0:T(128)S(1)}, f32[16]{0:T(128)S(1)}) all-reduce(f32[16]{0:T(128)S(1)} %get-tuple-element.415, f32[16]{0:T(128)S(1)} %get-tuple-element.414), channel_id=1, replica_groups=mesh['leaf'=8,'probe'=4] {'leaf'}, use_global_device_ids=true, to_apply=%region_1.2 | all-reduce | flops 32 | bytes 256 | tf_op jit(solution)/shard_map/psum | solution.py:51
  202.4 17.1 %psum.30 = f32[16]{0:T(128)S(1)} all-reduce(f32[16]{0:T(128)S(1)} %multiply_reduce_fusion.3), channel_id=1, replica_groups=mesh['leaf'=8,'probe'=4] {'leaf'}, use_global_device_ids=true, to_apply=%region_9.12 | all-reduce | flops 16 | bytes 128 | tf_op jit(solution)/shard_map/psum | solution.py:97
  222.6 6.0 %collective-permute-done.3 = f32[16,5,256]{2,1,0:T(8,128)S(1)} collective-permute-done((f32[16,5,256]{2,1,0:T(8,128)S(1)}, f32[16,5,256]{2,1,0:T(8,128)S(1)}, u32[]{:S(2)}, u32[]{:S(2)}) %collective-permute-start.3) | collective-permute-done | bytes 81952 | tf_op jit(solution)/shard_map/ppermute | solution.py:21
  228.6 7.9 %all_gather.15 = f32[64,5,256]{2,0,1:T(8,128)S(1)} all-gather(f32[16,5,256]{2,0,1:T(8,128)S(1)} %copy.58), channel_id=1, replica_groups=mesh['leaf'=8,'probe'=4] {'probe'}, dimensions={0}, use_global_device_ids=true | all-gather | bytes 409600 | tf_op jit(solution)/shard_map/all_gather | solution.py:55
  240.1 43.8 %while.29 = (s32[]{:T(128)}, f32[64,21,256]{2,1,0:T(8,128)S(1)}, s32[]{:T(128)}, s32[]{:T(128)}, s32[96]{0:T(128)S(1)}, /*index=5*/s32[96]{0:T(128)S(1)}, f32[64...) while((s32[]{:T(128)}, f32[64,21,256]{2,1,0:T(8,128)S(1)}, ...), condition=%wide.region_12.15_spmd.clone.clone, body=%wide.region_10.14_spmd.clone.clone.sunk | while | flops 891337280 | bytes 17392616 | solution.py:86
  246.6 5.1 %convolution_bitcast_fusion.5 = f32[64,8,256]{2,0,1:T(8,128)S(1)} fusion(f32[8,64,256]{2,1,0:T(8,128)S(1)} %gather_fusion.4, pred[8]{0:T(512)(128)(4,1)S(1)} %compare_and_fusion.11, f32[8,256,256]{2,1,0:T(8,128)} %multiply_reduce_fusion.9, f32[8]{0:T(128)S(1)} %get-tuple-element.592), kind=kOutput, calls=%fused_computation.51.clone.1 | convolution fusion | flops 410124288 | bytes 3145768 | tf_op jit(solution)/shard_map/while/body/bak,cbk->cba/dot_general | solution.py:68
  255.5 4.7 %fusion.76 = f32[64,8,256]{2,0,1:T(8,128)S(1)} fusion(f32[8,64,256]{2,1,0:T(8,128)} %gather_fusion.7, f32[8]{0:T(128)S(1)} %get-tuple-element.593, pred[8]{0:T(512)(128)(4,1)S(1)} %compare_and_fusion.12, f32[8,256,256]{2,1,0:T(8,128)} %multiply_reduce_fusion.9, f32[8]{0:T(128)S(1)} %get-tuple-element.592), kind=kOutput, calls=%fused_computation.53.clone.1 | convolution fusion | flops 410255360 | bytes 3145800 | tf_op jit(solution)/shard_map/while/body/bak,cba->cbk/dot_general | solution.py:72
  268.5 5.1 %convolution_bitcast_fusion.5 = f32[64,8,256]{2,0,1:T(8,128)S(1)} fusion(f32[8,64,256]{2,1,0:T(8,128)S(1)} %gather_fusion.4, pred[8]{0:T(512)(128)(4,1)S(1)} %compare_and_fusion.11, f32[8,256,256]{2,1,0:T(8,128)} %multiply_reduce_fusion.9, f32[8]{0:T(128)S(1)} %get-tuple-element.592), kind=kOutput, calls=%fused_computation.51.clone.1 | convolution fusion | flops 410124288 | bytes 3145768 | tf_op jit(solution)/shard_map/while/body/bak,cbk->cba/dot_general | solution.py:68
  277.4 4.7 %fusion.76 = f32[64,8,256]{2,0,1:T(8,128)S(1)} fusion(f32[8,64,256]{2,1,0:T(8,128)} %gather_fusion.7, f32[8]{0:T(128)S(1)} %get-tuple-element.593, pred[8]{0:T(512)(128)(4,1)S(1)} %compare_and_fusion.12, f32[8,256,256]{2,1,0:T(8,128)} %multiply_reduce_fusion.9, f32[8]{0:T(128)S(1)} %get-tuple-element.592), kind=kOutput, calls=%fused_computation.53.clone.1 | convolution fusion | flops 410255360 | bytes 3145800 | tf_op jit(solution)/shard_map/while/body/bak,cba->cbk/dot_general | solution.py:72
  285.0 46.9 %reduce-scatter.5.cloned.1.call-done = f32[16,21,256]{2,1,0:T(8,128)} async-done(((f32[64,21,256]{2,1,0:T(8,128)}), f32[16,21,256]{2,1,0:T(8,128)}) %reduce-scatter.5.cloned.1.call-update) | async-done | bytes 344080 | tf_op jit(solution)/shard_map/reduce_scatter | solution.py:87
  332.8 3.4 collective-permute-start.4
  340.2 22.4 %psum.31 = f32[16]{0:T(128)S(1)} all-reduce(f32[16]{0:T(128)S(1)} %multiply_reduce_fusion.2), channel_id=1, replica_groups=mesh['leaf'=8,'probe'=4] {'leaf'}, use_global_device_ids=true, to_apply=%region_15.18 | all-reduce | flops 16 | bytes 128 | tf_op jit(solution)/shard_map/psum | solution.py:92
  (142 shorter events, 74.4 us)
Async XLA Ops:
  7.2 5.6 %copy-start.6 = (s32[16,256]{1,0:T(8,128)S(1)}, s32[16,256]{1,0:T(8,128)}, u32[]{:S(2)}) copy-start(s32[16,256]{1,0:T(8,128)} %param.14) | copy-start | bytes 49156
  7.2 66.7 %all-gather.3.cloned.1.call-start = ((), (), s32[]{:S(2)}) async-start(), calls=%async_computation.2 | async-start | bytes 1310720 | tf_op jit(solution)/shard_map/all_gather | solution.py:54
  9.0 162.5 %reduce-scatter.3.cloned.1.call-start = ((), (), s32[]{:S(2)}) async-start(), calls=%async_computation.3 | async-start | bytes 1966080 | tf_op jit(solution)/shard_map/reduce_scatter | solution.py:87
  9.9 57.1 %collective-permute-start = (f32[16,5,256]{2,1,0:T(8,128)S(1)}, f32[16,5,256]{2,1,0:T(8,128)S(1)}, u32[]{:S(2)}, u32[]{:S(2)}) collective-permute-start(f32[16,5,256]{2,1,0:T(8,128)S(1)} %slice.68), channel_id=1, source_target_pairs={{4,0},{8,4},{12,8},{16,12},{20,16},{24,20},{28,24},{5,1},{9,5},{13... | collective-permute-start | bytes 245768 | tf_op jit(solution)/shard_map/ppermute | solution.py:21
  12.8 48.2 %copy-start.7 = (s32[2,96]{1,0:T(2,128)S(1)}, s32[2,96]{1,0:T(2,128)}, u32[]{:S(2)}) copy-start(s32[2,96]{1,0:T(2,128)} %param.15) | copy-start | bytes 2308
  59.7 7.3 %collective-permute-start.1 = (f32[3,5,256]{2,0,1:T(4,128)S(1)}, f32[3,5,256]{2,0,1:T(4,128)S(1)}, u32[]{:S(2)}, u32[]{:S(2)}) collective-permute-start(f32[3,5,256]{2,0,1:T(4,128)S(1)} %slice.69), channel_id=1, source_target_pairs={{4,0},{8,4},{12,8},{16,12},{20,16},{24,20},{28,24},{5,1},{9,5},{13... | collective-permute-start | bytes 46088 | tf_op jit(solution)/shard_map/ppermute | solution.py:21
  120.8 1.2 copy-start.1
  120.8 58.7 %copy-start.2 = (f32[16,4096]{1,0:T(8,128)S(1)}, f32[16,4096]{1,0:T(8,128)}, u32[]{:S(2)}) copy-start(f32[16,4096]{1,0:T(8,128)} %param.17) | copy-start | bytes 786436
  122.0 97.5 %copy-start.5 = (f32[2,8,16,256]{3,2,1,0:T(8,128)S(1)}, f32[2,8,16,256]{3,2,1,0:T(8,128)}, u32[]{:S(2)}) copy-start(f32[2,8,16,256]{3,2,1,0:T(8,128)} %copy.61) | copy-start | bytes 786436
  122.0 115.1 %all-gather.5.cloned.1.call-start = ((), (), s32[]{:S(2)}) async-start(), calls=%async_computation.4 | async-start | bytes 1310720 | tf_op jit(solution)/shard_map/all_gather | solution.py:54
  172.4 6.0 %collective-permute-start.2 = (f32[16,5,256]{2,1,0:T(8,128)S(1)}, f32[16,5,256]{2,1,0:T(8,128)S(1)}, u32[]{:S(2)}, u32[]{:S(2)}) collective-permute-start(f32[16,5,256]{2,1,0:T(8,128)S(1)} %slice.71), channel_id=1, source_target_pairs={{0,4},{4,8},{8,12},{12,16},{16,20},{20,24},{24,28},{1,5},{5,9},{9,... | collective-permute-start | bytes 245768 | tf_op jit(solution)/shard_map/ppermute | solution.py:21
  179.5 58.9 %copy-start.3 = (f32[2,8,16,256]{3,1,2,0:T(8,128)}, f32[2,8,16,256]{3,1,2,0:T(8,128)S(1)}, u32[]{:S(2)}) copy-start(f32[2,8,16,256]{3,1,2,0:T(8,128)S(1)} %copy.63) | copy-start | bytes 786436
  220.3 111.6 %reduce-scatter.5.cloned.1.call-start = ((), (), s32[]{:S(2)}) async-start(), calls=%async_computation.5 | async-start | bytes 1966080 | tf_op jit(solution)/shard_map/reduce_scatter | solution.py:87
  221.3 7.3 %collective-permute-start.3 = (f32[16,5,256]{2,1,0:T(8,128)S(1)}, f32[16,5,256]{2,1,0:T(8,128)S(1)}, u32[]{:S(2)}, u32[]{:S(2)}) collective-permute-start(f32[16,5,256]{2,1,0:T(8,128)S(1)} %slice.73), channel_id=1, source_target_pairs={{4,0},{8,4},{12,8},{16,12},{20,16},{24,20},{28,24},{5,1},{9,5},{13... | collective-permute-start | bytes 245768 | tf_op jit(solution)/shard_map/ppermute | solution.py:21
  283.8 1.2 copy-start
  283.8 56.1 %copy-start.4 = (f32[2,8,16,256]{3,1,2,0:T(8,128)S(1)}, f32[2,8,16,256]{3,1,2,0:T(8,128)}, u32[]{:S(2)}) copy-start(f32[2,8,16,256]{3,1,2,0:T(8,128)} %copy-done.3) | copy-start | bytes 786436
  332.8 6.0 %collective-permute-start.4 = (f32[16,5,256]{2,1,0:T(8,128)S(1)}, f32[16,5,256]{2,1,0:T(8,128)S(1)}, u32[]{:S(2)}, u32[]{:S(2)}) collective-permute-start(f32[16,5,256]{2,1,0:T(8,128)S(1)} %slice.75), channel_id=1, source_target_pairs={{0,4},{4,8},{8,12},{12,16},{16,20},{20,24},{24,28},{1,5},{5,9},{9,... | collective-permute-start | bytes 245768 | tf_op jit(solution)/shard_map/ppermute | solution.py:21
Sparse Core Ops, SparseCore 0:
  10.1 19.4 all-gather.2
  122.1 49.3 reduce-scatter.2
  220.5 16.5 all-gather.4
  285.1 46.7 reduce-scatter.4
where the time goes:
time: 374 us; the launch traced here: 370 us
  waiting for transfers between devices  111 us (30%)
  local copies, waits for them, and re-layouts  85.3 us (23%)
  blocking collectives  76.4 us (20%)
  matrix products  50.4 us (13%)
  other arithmetic  20.7 us (6%)
  between operations  14.8 us (4%)
  starting transfers between devices  10.8 us (3%)
    reduce_scatter x2, waiting for transfers between devices, body(): reduced = lax.psum_scatter(summed, 'probe', scatter_dimension=0, tiled=True)  96.3 us
    gather x2, local copies, waits for them, and re-layouts, body(): jnp.take_along_axis(coords.reshape(3, leaf_dev, width), site_order[None],...  46.8 us
    psum x1, blocking collectives, body(): norm_now = lax.psum(jnp.sum(residual * residual, axis=(1, 2)), 'leaf')  22.4 us
    psum x1, blocking collectives, body(): curve = lax.psum(jnp.sum(direction * image, axis=(1, 2)), 'leaf')  22.4 us
    dot_general x4, matrix products, one_block(): jnp.einsum('bak,cbk->cba', tiles, jnp.take(values, cols, axis=1), precisi...  20.6 us
    dot_general x4, matrix products, one_block(): jnp.einsum('bak,cba->cbk', tiles, jnp.take(values, rows, axis=1), precisi...  19 us
    psum x1, blocking collectives, body(): norm_next = lax.psum(jnp.sum(residual * residual, axis=(1, 2)), 'leaf')  17.1 us
    all_gather x2, blocking collectives, body(): far = lax.all_gather(rim, 'probe', axis=0, tiled=True)  14.5 us
  transfers between devices with their start and end apart: 9, of which 7 were waited for; matrix products, arithmetic and copies ran while one was open for 14% of the time, Pallas kernels for 0%

commit v1 on v0

v1 whole, which is shorter than its diff:
```python
import functools
import math

import jax
import jax.numpy as jnp
from jax import lax
from jax.experimental import pallas as pl
from jax.experimental.pallas import tpu as pltpu
from jax.sharding import PartitionSpec as P

REACH = 5
UNIT = 0.025
LENGTH = 0.12
NUGGET = 0.5
TAPER = REACH * UNIT
GROW = math.sqrt(3.0) * TAPER / LENGTH
QUAD = 4.0 * GROW
LIN = (4.0 + GROW) / QUAD
RATE = -GROW / math.log(2.0)
OFFS = REACH + 1
ROWS = 32
MESH = pl.DeviceIdType.MESH
F32 = jnp.float32
BF16 = jnp.bfloat16


def split(x):
    hi = x.astype(BF16)
    return hi, (x - hi.astype(F32)).astype(BF16)


def stacked(x):
    hi = x.astype(BF16).astype(F32)
    return jnp.concatenate([hi, x - hi], axis=0).astype(BF16)


def dot(a, b, ca, cb):
    return lax.dot_general(a, b, (((ca,), (cb,)), ((), ())), preferred_element_type=F32)


def fold(x):
    half = x.shape[0] // 2
    return x[:half] + x[half:]


def kernel(
    n, coords_ref, order_ref, pairs_ref, count_ref, probes_ref, sol_ref, res_ref,
    c8, prow, pcb, mask, tiles, v, v2, acc, r1, acc2, halo0, back0, back1, halo1,
    sum_out, sum_in, ssem, rsem, hsend, hrecv,
):
    leaf_dev, width = order_ref.shape
    cols = probes_ref.shape[0]
    extent = leaf_dev + REACH
    me = lax.axis_index("leaf")
    after = lax.rem(me + 1, n)
    before = lax.rem(me + n - 1, n)

    barrier = pltpu.get_barrier_semaphore()
    for k in range(1, n):
        pl.semaphore_signal(
            barrier, inc=1, device_id={"leaf": lax.rem(me + k, n)}, device_id_type=MESH
        )

    c8[...] = jnp.zeros_like(c8)
    c8[0:3, :] = coords_ref[...] * (1.0 / TAPER)
    place = lax.broadcasted_iota(jnp.int32, (width, width), 0)

    for l in range(leaf_dev):
        x = c8[:, l * width : (l + 1) * width]
        hi = x.astype(BF16).astype(F32)
        mid = (x - hi).astype(BF16).astype(F32)
        parts = jnp.concatenate([hi, mid, x - hi - mid], axis=0).astype(BF16)
        onehot = jnp.where(place == order_ref[l : l + 1, :], 1.0, 0.0).astype(BF16)
        got = dot(parts, onehot, 1, 0)
        prow[l] = got[0:8] + got[8:16] + got[16:24]

    slots = pairs_ref.shape[1]
    first = pairs_ref[0:1, :]
    second = pairs_ref[1:2, :]
    code = (first - me * leaf_dev) * OFFS + (second - first)
    lane = lax.broadcasted_iota(jnp.int32, (1, slots), 1)
    code = jnp.where(lane < count_ref[0], code, -1)
    want = lax.broadcasted_iota(jnp.int32, (leaf_dev * OFFS, slots), 0)
    hit = jnp.max(jnp.where(want == code, 1.0, 0.0), axis=1, keepdims=True)
    mask[...] = jnp.broadcast_to(hit, mask.shape)

    rr = jnp.zeros((cols, width), F32)
    for l in range(leaf_dev):
        x = probes_ref[:, l * width : (l + 1) * width]
        v[l] = x
        v2[l] = stacked(x)
        rr = rr + x * x
    acc[...] = jnp.zeros_like(acc)
    acc2[...] = jnp.zeros_like(acc2)

    pl.semaphore_wait(barrier, n - 1)

    def hop(src, dst, slot, to):
        return pltpu.make_async_remote_copy(
            src_ref=src, dst_ref=dst, send_sem=hsend.at[slot], recv_sem=hrecv.at[slot],
            device_id={"leaf": to}, device_id_type=MESH,
        )

    point_hop = hop(prow.at[pl.ds(0, REACH)], prow.at[pl.ds(leaf_dev, REACH)], 0, before)
    probe_hop = hop(probes_ref.at[:, pl.ds(0, REACH * width)], halo0, 1, before)
    point_hop.start()
    probe_hop.start()

    def products(i, get, into):
        vi = v2[i]
        row = jnp.zeros((width, 2 * cols), F32)
        for o in range(OFFS):
            hi, lo = get(i * OFFS + o, o)
            vj = v2[i + o]
            row = row + dot(hi, vj, 1, 1) + dot(lo, vj, 1, 1)
            if o > 0:
                into[i + o] += fold(dot(vi, hi, 1, 0) + dot(vi, lo, 1, 0))
        into[i] += fold(row.T)

    def build(i, s, o):
        for h in range(0, width, 128):
            listed = mask[pl.ds(s, 1), :]
            right = [
                jnp.broadcast_to(
                    jnp.where(
                        listed > 0.0,
                        prow[i + o, c : c + 1, h : h + 128],
                        prow[i, c : c + 1, h : h + 128],
                    ),
                    (ROWS, 128),
                )
                for c in range(3)
            ]
            top = jnp.broadcast_to(listed, (ROWS, 128))
            for a in range(0, width, ROWS):
                dx = pcb[0, a : a + ROWS, :] - right[0]
                dy = pcb[1, a : a + ROWS, :] - right[1]
                dz = pcb[2, a : a + ROWS, :] - right[2]
                d2 = jnp.maximum(dx * dx + dy * dy + dz * dz, 1e-30)
                u = d2 * lax.rsqrt(d2)
                w = jnp.maximum(top - u, 0.0)
                w = w * w
                w = w * w
                t = w * (d2 + (LIN * u + 1.0 / QUAD)) * jnp.exp2(RATE * u)
                hi, lo = split(t)
                tiles[s, 0, a : a + ROWS, h : h + 128] = hi
                tiles[s, 1, a : a + ROWS, h : h + 128] = lo
        return tiles[s, 0], tiles[s, 1]

    def first_pass(i, carry):
        @pl.when(i == leaf_dev - REACH)
        def _():
            point_hop.wait_recv()
            probe_hop.wait_recv()
            for k in range(REACH):
                x = halo0[:, k * width : (k + 1) * width]
                v[leaf_dev + k] = x
                v2[leaf_dev + k] = stacked(x)

        turned = prow[i].T
        for c in range(3):
            pcb[c] = jnp.broadcast_to(turned[:, c : c + 1], (width, 128))
        products(i, lambda s, o: build(i, s, o), acc)
        return carry

    lax.fori_loop(0, leaf_dev, first_pass, 0)

    lanes = lax.broadcasted_iota(jnp.int32, (cols, 128), 1)

    def share(which, *parts):
        packed = jnp.zeros((cols, 128), F32)
        for k, part in enumerate(parts):
            total = jnp.sum(part, axis=1, keepdims=True)
            packed = jnp.where(lanes == k, total, packed)
        sum_out[which] = packed
        copies = []
        for k in range(1, n):
            slot = which * (n - 1) + k - 1
            copy = pltpu.make_async_remote_copy(
                src_ref=sum_out.at[which], dst_ref=sum_in.at[slot],
                send_sem=ssem.at[slot], recv_sem=rsem.at[slot],
                device_id={"leaf": lax.rem(me + k, n)}, device_id_type=MESH,
            )
            copy.start()
            copies.append(copy)
        return packed, copies

    def collect(which, packed, copies):
        total = packed
        for k, copy in enumerate(copies):
            copy.wait()
            total = total + sum_in[which * (n - 1) + k]
        return total

    back0_hop = hop(acc.at[pl.ds(leaf_dev, REACH)], back0, 2, after)
    back0_hop.start()
    dq = (NUGGET / QUAD) * rr
    for l in range(extent):
        dq = dq + v[l] * acc[l]
    packed, copies = share(0, rr, dq)
    total = collect(0, packed, copies)
    rr0 = total[:, 0:1]
    dq0 = total[:, 1:2] * QUAD
    alpha0 = rr0 / dq0
    back0_hop.wait_recv()

    rr1 = jnp.zeros((cols, width), F32)
    rq = jnp.zeros((cols, width), F32)
    halo_hop = hop(r1.at[pl.ds(0, REACH)], halo1, 3, before)
    for l in range(leaf_dev):
        d = v[l]
        sums = acc[l] + back0[l] if l < REACH else acc[l]
        q = NUGGET * d + QUAD * sums
        r = d - alpha0 * q
        acc[l] = q
        r1[l] = r
        v2[l] = stacked(r)
        rr1 = rr1 + r * r
        rq = rq + r * q
        if l == REACH - 1:
            halo_hop.start()

    def second_pass(i, carry):
        @pl.when(i == leaf_dev - REACH)
        def _():
            halo_hop.wait_recv()
            for k in range(REACH):
                v2[leaf_dev + k] = stacked(halo1[k])

        products(i, lambda s, o: (tiles[s, 0], tiles[s, 1]), acc2)
        return carry

    lax.fori_loop(0, leaf_dev, second_pass, 0)

    back1_hop = hop(acc2.at[pl.ds(leaf_dev, REACH)], back1, 4, after)
    back1_hop.start()
    rw = (NUGGET / QUAD) * rr1
    for l in range(leaf_dev):
        rw = rw + r1[l] * acc2[l]
    for k in range(REACH):
        rw = rw + halo1[k] * acc2[leaf_dev + k]
    packed, copies = share(1, rr1, rw, rq)
    total = collect(1, packed, copies)
    new = total[:, 0:1]
    beta = new / rr0
    curve = total[:, 1:2] * QUAD + beta * (2.0 * total[:, 2:3] + beta * dq0)
    alpha1 = new / curve
    back1_hop.wait_recv()
    for l in range(leaf_dev):
        d = v[l]
        r = r1[l]
        sums = acc2[l] + back1[l] if l < REACH else acc2[l]
        q = NUGGET * r + QUAD * sums + beta * acc[l]
        sol_ref[:, l * width : (l + 1) * width] = alpha0 * d + alpha1 * (r + beta * d)
        res_ref[:, l * width : (l + 1) * width] = r - alpha1 * q
    for copy in (point_hop, probe_hop, back0_hop, halo_hop, back1_hop):
        copy.wait_send()


def body(coords, site_order, leaf_pairs, pair_count, probes):
    n = lax.axis_size("leaf")
    leaf_dev, width = site_order.shape
    cols = probes.shape[0]
    extent = leaf_dev + REACH
    slots = leaf_dev * OFFS
    vmem = pl.BlockSpec(memory_space=pltpu.VMEM)
    smem = pl.BlockSpec(memory_space=pltpu.SMEM)
    field = functools.partial(pltpu.VMEM, dtype=F32)
    return pl.pallas_call(
        functools.partial(kernel, n),
        out_shape=(jax.ShapeDtypeStruct(probes.shape, F32),) * 2,
        in_specs=[vmem, vmem, vmem, smem, vmem],
        out_specs=(vmem, vmem),
        scratch_shapes=[
            field((8, leaf_dev * width)),
            field((extent, 8, width)),
            field((3, width, 128)),
            field((slots, 128)),
            pltpu.VMEM((slots, 2, width, width), BF16),
            field((extent, cols, width)),
            pltpu.VMEM((extent, 2 * cols, width), BF16),
            field((extent, cols, width)),
            field((leaf_dev, cols, width)),
            field((extent, cols, width)),
            field((cols, REACH * width)),
            field((REACH, cols, width)),
            field((REACH, cols, width)),
            field((REACH, cols, width)),
            field((2, cols, 128)),
            field((2 * (n - 1), cols, 128)),
            pltpu.SemaphoreType.DMA((2 * (n - 1),)),
            pltpu.SemaphoreType.DMA((2 * (n - 1),)),
            pltpu.SemaphoreType.DMA((5,)),
            pltpu.SemaphoreType.DMA((5,)),
        ],
        compiler_params=pltpu.CompilerParams(
            collective_id=0, has_side_effects=True, vmem_limit_bytes=56 * 2**20
        ),
    )(coords, site_order, leaf_pairs, pair_count, probes)


def solution(mesh):
    in_specs = (P(None, "leaf"), P("leaf", None), P(None, "leaf"), P("leaf"), P("probe", "leaf"))
    out_specs = (P("probe", "leaf"), P("probe", "leaf"))
    return jax.shard_map(body, mesh=mesh, in_specs=in_specs, out_specs=out_specs, check_vma=False)
```

time: 374 us -> 66.1 us (0.18)
  waiting for transfers between devices: 111 us -> 0 us
  local copies, waits for them, and re-layouts: 85.3 us -> 2.42 us
  blocking collectives: 76.4 us -> 0 us
  Pallas kernels: 0 us -> 62.2 us
  matrix products: 50.4 us -> 0 us
  other arithmetic: 20.7 us -> 0 us
  between operations: 14.8 us -> 1.29 us
  starting transfers between devices: 10.8 us -> 0 us
    reduce_scatter x2 -> x0, waiting for transfers between devices: 96.3 us -> none  [body(): reduced = lax.psum_scatter(summed, 'probe', scatter_dimension=0, tiled=True)]
    gather x18 -> x0, local copies, waits for them, and re-layouts: 70 us -> none  [the longest x2 46.8 us: body(): jnp.take_along_axis(coords.reshape(3, leaf_dev, width), site_order[None],...]
    pallas_call x0 -> x1, Pallas kernels: none -> 62.2 us  [body(): pl.pallas_call(functools.partial(kernel, n), out_shape=(jax.ShapeDtypeStr...]
    psum x3 -> x0, blocking collectives: 61.9 us -> none  [the longest x1 22.4 us: body(): norm_now = lax.psum(jnp.sum(residual * residual, axis=(1, 2)), 'leaf')]
    dot_general x16 -> x0, matrix products: 50.4 us -> none  [the longest x4 20.6 us: one_block(): jnp.einsum('bak,cbk->cba', tiles, jnp.take(values, cols, axis=1), precisi...]
    all_gather x2 -> x0, blocking collectives: 14.5 us -> none  [body(): far = lax.all_gather(rim, 'probe', axis=0, tiled=True)]
    ppermute x5 -> x0, waiting for transfers between devices: 14.3 us -> none  [from_behind(): return lax.ppermute(value, axis, pairs)]
    ppermute x5 -> x0, starting transfers between devices: 10.7 us -> none  [from_behind(): return lax.ppermute(value, axis, pairs)]
  transfers between devices with their start and end apart: 9 -> 0, of which waited for: 7 -> 0; matrix products, arithmetic and copies ran while one was open for 14% -> 0% of each run, Pallas kernels for 0% -> 0%
where the time goes in v1:
time: 66.1 us; the launch traced here: 65.9 us
  Pallas kernels  62.2 us (94%)
  local copies, waits for them, and re-layouts  2.42 us (4%)
  between operations  1.29 us (2%)
    pallas_call x1, Pallas kernels, body(): pl.pallas_call(functools.partial(kernel, n), out_shape=(jax.ShapeDtypeStr...  62.2 us
    unnamed x4, local copies, waits for them, and re-layouts  2.42 us

profile of v1, /device:TPU:0, one launch (start us, length us, event | category | flops | bytes accessed | tf_op | source)
XLA Modules:
  0.0 65.9 jit_solution(214475106002019756)
XLA Ops:
  1.3 62.2 %shard_map.68 = (f32[16,4096]{1,0:T(8,128)}, f32[16,4096]{1,0:T(8,128)}) custom-call(f32[3,4096]{1,0:T(4,128)} %coords_ref.1, s32[16,256]{1,0:T(8,128)} %order_ref.1, s32[2,96]{1,0:T(2,128)} %pairs_ref.1, s32[1]{0:T(128)S(6)} %copy.9.count_ref, f32[16,4096]{1,0:T(8,128)} %probes_ref.1), custom_call_target="tpu_custom_call" | custom-call | tf_op jit(solution)/shard_map/pallas_call | solution.py:269
  63.5 0.0 copy-start
  63.5 1.7 %copy.10 = f32[16,4096]{1,0:T(8,128)} copy(f32[16,4096]{1,0:T(8,128)} %get-tuple-element.4) | data formatting | bytes 524288
  65.2 0.0 copy-done
  65.2 0.7 %copy.11 = f32[16,4096]{1,0:T(8,128)} copy(f32[16,4096]{1,0:T(8,128)S(1)} %copy-done) | data formatting | bytes 524288
Async XLA Ops:
  63.5 1.7 %copy-start = (f32[16,4096]{1,0:T(8,128)S(1)}, f32[16,4096]{1,0:T(8,128)}, u32[]{:S(2)}) copy-start(f32[16,4096]{1,0:T(8,128)} %get-tuple-element.5) | copy-start | bytes 786436

commit v2 on v1

v2 whole, which is shorter than its diff:
```python
import functools
import math

import jax
import jax.numpy as jnp
from jax import lax
from jax.experimental import pallas as pl
from jax.experimental.pallas import tpu as pltpu
from jax.sharding import PartitionSpec as P

REACH = 5
UNIT = 0.025
LENGTH = 0.12
NUGGET = 0.5
TAPER = REACH * UNIT
GROW = math.sqrt(3.0) * TAPER / LENGTH
QUAD = 4.0 * GROW
LIN = (4.0 + GROW) / QUAD
RATE = -GROW / math.log(2.0)
OFFS = REACH + 1
ROWS = 32
MESH = pl.DeviceIdType.MESH
F32 = jnp.float32
BF16 = jnp.bfloat16


def split(x):
    hi = x.astype(BF16)
    return hi, (x - hi.astype(F32)).astype(BF16)


def stacked(x):
    hi = x.astype(BF16).astype(F32)
    return jnp.concatenate([hi, x - hi], axis=0).astype(BF16)


def dot(a, b, ca, cb):
    return lax.dot_general(a, b, (((ca,), (cb,)), ((), ())), preferred_element_type=F32)


def fold(x):
    half = x.shape[0] // 2
    return x[:half] + x[half:]


def kernel(
    n, coords_ref, order_ref, pairs_ref, count_ref, probes_ref, sol_ref, res_ref,
    c8, prow, pcb, mask, tiles, v, v2, acc, r1, acc2, twin0, twin1, halo0, halo1,
    part0, part1, back0, back1, sum_out, sum_in, ssem, rsem, hsend, hrecv,
):
    leaf_dev, width = order_ref.shape
    cols = probes_ref.shape[0]
    half = leaf_dev // 2
    span = half + REACH
    me = lax.axis_index("leaf")
    probe = lax.axis_index("probe")
    mine = lax.rem(probe, 2)
    other = 1 - mine
    even = probe - mine
    twin = even + other
    base = half * mine
    twin_base = half * other
    after = lax.rem(me + 1, n)
    before = lax.rem(me + n - 1, n)

    peers = [(k - 1, lax.rem(me + k, n), probe, mine) for k in range(1, n)]
    peers += [(n - 1 + k, lax.rem(me + k, n), twin, other) for k in range(n)]
    slots_in = len(peers)

    barrier = pltpu.get_barrier_semaphore()
    for _, leaf, row, _ in peers:
        pl.semaphore_signal(
            barrier, inc=1, device_id={"leaf": leaf, "probe": row}, device_id_type=MESH
        )

    rr = jnp.zeros((cols, width), F32)
    for l in range(leaf_dev):
        x = probes_ref[:, l * width : (l + 1) * width]
        v[mine, l] = x
        rr = rr + x * x
    v[mine, pl.ds(leaf_dev, REACH)] = jnp.zeros((REACH, cols, width), F32)

    c8[...] = jnp.zeros_like(c8)
    c8[0:3, :] = coords_ref[...] * (1.0 / TAPER)
    place = lax.broadcasted_iota(jnp.int32, (width, width), 0)

    for l in range(leaf_dev):
        x = c8[:, l * width : (l + 1) * width]
        hi = x.astype(BF16).astype(F32)
        mid = (x - hi).astype(BF16).astype(F32)
        parts = jnp.concatenate([hi, mid, x - hi - mid], axis=0).astype(BF16)
        onehot = jnp.where(place == order_ref[l : l + 1, :], 1.0, 0.0).astype(BF16)
        got = dot(parts, onehot, 1, 0)
        prow[l] = got[0:8] + got[8:16] + got[16:24]

    pl.semaphore_wait(barrier, slots_in)

    def hop(src, dst, slot, leaf, row, landing=None):
        return pltpu.make_async_remote_copy(
            src_ref=src, dst_ref=dst, send_sem=hsend.at[slot],
            recv_sem=hrecv.at[slot if landing is None else landing],
            device_id={"leaf": leaf, "probe": row}, device_id_type=MESH,
        )

    twin0_hop = hop(v.at[mine, pl.ds(twin_base, span)], twin0, 0, me, twin)
    point_hop = hop(prow.at[pl.ds(0, REACH)], prow.at[pl.ds(leaf_dev, REACH)], 1, before, probe)
    rim0_hop = hop(v.at[mine, pl.ds(0, REACH)], halo0.at[mine], 2, before, even + 1, 2 + mine)
    rim0_in = [
        hop(v.at[mine, pl.ds(0, REACH)], halo0.at[k], 2, before, even + 1, 2 + k) for k in range(2)
    ]
    twin0_hop.start()
    point_hop.start()
    rim0_hop.start()

    slots = pairs_ref.shape[1]
    first = pairs_ref[0:1, :]
    second = pairs_ref[1:2, :]
    code = (first - me * leaf_dev) * OFFS + (second - first)
    lane = lax.broadcasted_iota(jnp.int32, (1, slots), 1)
    code = jnp.where(lane < count_ref[0], code, -1)
    want = lax.broadcasted_iota(jnp.int32, (leaf_dev * OFFS, slots), 0)
    hit = jnp.max(jnp.where(want == code, 1.0, 0.0), axis=1, keepdims=True)
    mask[...] = jnp.broadcast_to(hit, mask.shape)
    acc[...] = jnp.zeros_like(acc)
    acc2[...] = jnp.zeros_like(acc2)

    def both(field, l):
        return stacked(jnp.concatenate([field[0, l], field[1, l]], axis=0))

    def accept(field, twins):
        for k in range(span):
            field[other, base + k] = twins[k]
        for k in range(span):
            v2[base + k] = both(field, base + k)

    def accept_rim(field, halo):
        for k in range(REACH):
            for r in range(2):
                field[r, leaf_dev + k] = halo[r, k]
            v2[leaf_dev + k] = both(field, leaf_dev + k)

    def add(into, l, x):
        x = fold(x)
        into[0, l] += x[:cols]
        into[1, l] += x[cols:]

    def products(i, get, into):
        vi = v2[i]
        row = jnp.zeros((width, 4 * cols), F32)
        for o in range(OFFS):
            hi, lo = get((i - base) * OFFS + o, o)
            vj = v2[i + o]
            row = row + dot(hi, vj, 1, 1) + dot(lo, vj, 1, 1)
            if o > 0:
                add(into, i + o, dot(vi, hi, 1, 0) + dot(vi, lo, 1, 0))
        add(into, i, row.T)

    def build(i, s, o):
        for h in range(0, width, 128):
            listed = mask[pl.ds(i * OFFS + o, 1), :]
            right = [
                jnp.broadcast_to(
                    jnp.where(
                        listed > 0.0,
                        prow[i + o, c : c + 1, h : h + 128],
                        prow[i, c : c + 1, h : h + 128],
                    ),
                    (ROWS, 128),
                )
                for c in range(3)
            ]
            top = jnp.broadcast_to(listed, (ROWS, 128))
            for a in range(0, width, ROWS):
                dx = pcb[0, a : a + ROWS, :] - right[0]
                dy = pcb[1, a : a + ROWS, :] - right[1]
                dz = pcb[2, a : a + ROWS, :] - right[2]
                d2 = jnp.maximum(dx * dx + dy * dy + dz * dz, 1e-30)
                u = d2 * lax.rsqrt(d2)
                w = jnp.maximum(top - u, 0.0)
                w = w * w
                w = w * w
                t = w * (d2 + (LIN * u + 1.0 / QUAD)) * jnp.exp2(RATE * u)
                hi, lo = split(t)
                tiles[s, 0, a : a + ROWS, h : h + 128] = hi
                tiles[s, 1, a : a + ROWS, h : h + 128] = lo
        return tiles[s, 0], tiles[s, 1]

    twin0_hop.wait_recv()
    accept(v, twin0)

    def first_pass(i, carry):
        @pl.when(i == leaf_dev - REACH)
        def _():
            point_hop.wait_recv()
            for k in range(2):
                rim0_in[k].wait_recv()
            accept_rim(v, halo0)

        turned = prow[i].T
        for c in range(3):
            pcb[c] = jnp.broadcast_to(turned[:, c : c + 1], (width, 128))
        products(i, lambda s, o: build(i, s, o), acc)
        return carry

    lax.fori_loop(base, base + half, first_pass, 0)

    @pl.when(mine == 0)
    def _():
        point_hop.wait_recv()

    lanes = lax.broadcasted_iota(jnp.int32, (cols, 128), 1)

    def overlap(field, sums):
        totals = []
        for r in range(2):
            x = jnp.zeros((cols, width), F32)
            for k in range(span):
                x = x + field[r, base + k] * sums[r, base + k]
            totals.append(jnp.sum(x, axis=1, keepdims=True))
        return totals

    def share(which, shared, own):
        own = [jnp.sum(x, axis=1, keepdims=True) for x in own]
        for r in range(2):
            keep = jnp.where(mine == r, 1.0, 0.0)
            packed = jnp.where(lanes == 0, shared[r], 0.0)
            for k, x in enumerate(own):
                packed = jnp.where(lanes == k + 1, x * keep, packed)
            sum_out[which, r] = packed
        copies = []
        for slot, leaf, row, side in peers:
            at = which * slots_in + slot
            copy = pltpu.make_async_remote_copy(
                src_ref=sum_out.at[which, side], dst_ref=sum_in.at[at],
                send_sem=ssem.at[at], recv_sem=rsem.at[at],
                device_id={"leaf": leaf, "probe": row}, device_id_type=MESH,
            )
            copy.start()
            copies.append(copy)
        return copies

    def collect(which, copies):
        total = sum_out[which, mine]
        for k, copy in enumerate(copies):
            copy.wait()
            total = total + sum_in[which * slots_in + k]
        return total

    def give_back(sums, part, back, slot):
        whole = hop(sums.at[other, pl.ds(base, span)], part, slot, me, twin)
        rims = [
            hop(sums.at[r, pl.ds(leaf_dev, REACH)], back, slot + 1 + r, after, even + r, slot + 1)
            for r in range(2)
        ]
        whole.start()

        @pl.when(mine == 1)
        def _():
            for rim in rims:
                rim.start()

        return whole, rims

    def take_back(sums, part, back, hops):
        whole, rims = hops
        whole.wait_recv()
        for k in range(span):
            sums[mine, twin_base + k] += part[k]
        rims[0].wait_recv()
        for k in range(REACH):
            sums[mine, k] += back[k]
        whole.wait_send()

        @pl.when(mine == 1)
        def _():
            for rim in rims:
                rim.wait_send()

    copies = share(0, overlap(v, acc), [rr])
    hops = give_back(acc, part0, back0, 4)
    total = collect(0, copies)
    rr0 = total[:, 1:2]
    dq0 = total[:, 0:1] * QUAD + NUGGET * rr0
    alpha0 = rr0 / dq0
    take_back(acc, part0, back0, hops)

    rr1 = jnp.zeros((cols, width), F32)
    rq = jnp.zeros((cols, width), F32)
    for l in range(leaf_dev):
        d = v[mine, l]
        q = NUGGET * d + QUAD * acc[mine, l]
        r = d - alpha0 * q
        acc[mine, l] = q
        r1[mine, l] = r
        rr1 = rr1 + r * r
        rq = rq + r * q
    r1[mine, pl.ds(leaf_dev, REACH)] = jnp.zeros((REACH, cols, width), F32)
    twin1_hop = hop(r1.at[mine, pl.ds(twin_base, span)], twin1, 7, me, twin)
    rim1_hop = hop(r1.at[mine, pl.ds(0, REACH)], halo1.at[mine], 8, before, even + 1, 8 + mine)
    rim1_in = [
        hop(r1.at[mine, pl.ds(0, REACH)], halo1.at[k], 8, before, even + 1, 8 + k) for k in range(2)
    ]
    twin1_hop.start()
    rim1_hop.start()
    twin1_hop.wait()
    accept(r1, twin1)

    def second_pass(i, carry):
        @pl.when(i == leaf_dev - REACH)
        def _():
            for k in range(2):
                rim1_in[k].wait_recv()
            accept_rim(r1, halo1)

        products(i, lambda s, o: (tiles[s, 0], tiles[s, 1]), acc2)
        return carry

    lax.fori_loop(base, base + half, second_pass, 0)

    copies = share(1, overlap(r1, acc2), [rr1, rq])
    hops = give_back(acc2, part1, back1, 10)
    total = collect(1, copies)
    new = total[:, 1:2]
    beta = new / rr0
    curve = total[:, 0:1] * QUAD + NUGGET * new + beta * (2.0 * total[:, 2:3] + beta * dq0)
    alpha1 = new / curve
    take_back(acc2, part1, back1, hops)
    for l in range(leaf_dev):
        d = v[mine, l]
        r = r1[mine, l]
        q = NUGGET * r + QUAD * acc2[mine, l] + beta * acc[mine, l]
        sol_ref[:, l * width : (l + 1) * width] = alpha0 * d + alpha1 * (r + beta * d)
        res_ref[:, l * width : (l + 1) * width] = r - alpha1 * q
    for copy in (twin0_hop, point_hop, rim0_hop, rim1_hop):
        copy.wait_send()


def body(coords, site_order, leaf_pairs, pair_count, probes):
    n = lax.axis_size("leaf")
    leaf_dev, width = site_order.shape
    cols = probes.shape[0]
    extent = leaf_dev + REACH
    span = leaf_dev // 2 + REACH
    slots_in = 2 * n - 1
    vmem = pl.BlockSpec(memory_space=pltpu.VMEM)
    smem = pl.BlockSpec(memory_space=pltpu.SMEM)
    field = functools.partial(pltpu.VMEM, dtype=F32)
    return pl.pallas_call(
        functools.partial(kernel, n),
        out_shape=(jax.ShapeDtypeStruct(probes.shape, F32),) * 2,
        in_specs=[vmem, vmem, vmem, smem, vmem],
        out_specs=(vmem, vmem),
        scratch_shapes=[
            field((8, leaf_dev * width)),
            field((extent, 8, width)),
            field((3, width, 128)),
            field((leaf_dev * OFFS, 128)),
            pltpu.VMEM((leaf_dev // 2 * OFFS, 2, width, width), BF16),
            field((2, extent, cols, width)),
            pltpu.VMEM((extent, 4 * cols, width), BF16),
            field((2, extent, cols, width)),
            field((2, extent, cols, width)),
            field((2, extent, cols, width)),
            field((span, cols, width)),
            field((span, cols, width)),
            field((2, REACH, cols, width)),
            field((2, REACH, cols, width)),
            field((span, cols, width)),
            field((span, cols, width)),
            field((REACH, cols, width)),
            field((REACH, cols, width)),
            field((2, 2, cols, 128)),
            field((2 * slots_in, cols, 128)),
            pltpu.SemaphoreType.DMA((2 * slots_in,)),
            pltpu.SemaphoreType.DMA((2 * slots_in,)),
            pltpu.SemaphoreType.DMA((13,)),
            pltpu.SemaphoreType.DMA((13,)),
        ],
        compiler_params=pltpu.CompilerParams(
            collective_id=0, has_side_effects=True, vmem_limit_bytes=48 * 2**20
        ),
    )(coords, site_order, leaf_pairs, pair_count, probes)


def solution(mesh):
    in_specs = (P(None, "leaf"), P("leaf", None), P(None, "leaf"), P("leaf"), P("probe", "leaf"))
    out_specs = (P("probe", "leaf"), P("probe", "leaf"))
    return jax.shard_map(body, mesh=mesh, in_specs=in_specs, out_specs=out_specs, check_vma=False)
```

time: 66.1 us -> 50.6 us (0.77)
  Pallas kernels: 62.2 us -> 44.9 us
  local copies, waits for them, and re-layouts: 2.42 us -> 3.92 us
    pallas_call x1, Pallas kernels: 62.2 us -> 44.9 us  [body(): pl.pallas_call(functools.partial(kernel, n), out_shape=(jax.ShapeDtypeStr...]
    unnamed x4 -> x10, local copies, waits for them, and re-layouts: 2.42 us -> 3.92 us
where the time goes in v2:
time: 50.6 us; the launch traced here: 50.1 us
  Pallas kernels  44.9 us (89%)
  local copies, waits for them, and re-layouts  3.92 us (8%)
  between operations  1.32 us (3%)
    pallas_call x1, Pallas kernels, body(): pl.pallas_call(functools.partial(kernel, n), out_shape=(jax.ShapeDtypeStr...  44.9 us
    unnamed x10, local copies, waits for them, and re-layouts  3.92 us

profile of v2, /device:TPU:0, one launch (start us, length us, event | category | flops | bytes accessed | tf_op | source)
XLA Modules:
  0.0 50.1 jit_solution(9205833938992862556)
XLA Ops:
  0.6 0.0 copy-start.3
  1.3 0.0 copy-done.3
  1.3 0.0 copy-start
  1.3 0.9 %copy-done = f32[16,4096]{1,0:T(8,128)S(1)} copy-done((f32[16,4096]{1,0:T(8,128)S(1)}, f32[16,4096]{1,0:T(8,128)}, u32[]{:S(2)}) %copy-start) | copy-done | bytes 262168
  2.3 0.0 copy-start.1
  2.3 0.8 %copy-done.1 = f32[3,4096]{1,0:T(4,128)S(1)} copy-done((f32[3,4096]{1,0:T(4,128)S(1)}, f32[3,4096]{1,0:T(4,128)}, u32[]{:S(2)}) %copy-start.1) | copy-done | bytes 49176
  3.1 0.0 copy-start.2
  3.1 0.7 %copy-done.2 = s32[16,256]{1,0:T(8,128)S(1)} copy-done((s32[16,256]{1,0:T(8,128)S(1)}, s32[16,256]{1,0:T(8,128)}, u32[]{:S(2)}) %copy-start.2) | copy-done | bytes 16408
  3.8 44.9 %shard_map.68 = (f32[16,4096]{1,0:T(8,128)S(1)}, f32[16,4096]{1,0:T(8,128)S(1)}) custom-call(f32[3,4096]{1,0:T(4,128)S(1)} %copy-done.1, s32[16,256]{1,0:T(8,128)S(1)} %copy-done.2, s32[2,96]{1,0:T(2,128)S(1)} %copy-done.3, s32[1]{0:T(128)S(6)} %copy.9.count_ref, f32[16,4096]{1,0:T(8,128)S(1)} %copy-done), custom_call_target="tpu_custom_call" | custom-call | tf_op jit(solution)/shard_map/pallas_call | solution.py:348
  48.7 0.7 %copy.10 = f32[16,4096]{1,0:T(8,128)} copy(f32[16,4096]{1,0:T(8,128)S(1)} %get-tuple-element.4) | data formatting | bytes 524288
  49.4 0.7 %copy.11 = f32[16,4096]{1,0:T(8,128)} copy(f32[16,4096]{1,0:T(8,128)S(1)} %get-tuple-element.5) | data formatting | bytes 524288
Async XLA Ops:
  0.6 0.7 %copy-start.3 = (s32[2,96]{1,0:T(2,128)S(1)}, s32[2,96]{1,0:T(2,128)}, u32[]{:S(2)}) copy-start(s32[2,96]{1,0:T(2,128)} %pairs_ref.1) | copy-start | bytes 2308
  1.3 0.9 %copy-start = (f32[16,4096]{1,0:T(8,128)S(1)}, f32[16,4096]{1,0:T(8,128)}, u32[]{:S(2)}) copy-start(f32[16,4096]{1,0:T(8,128)} %probes_ref.1) | copy-start | bytes 786436
  2.3 0.8 %copy-start.1 = (f32[3,4096]{1,0:T(4,128)S(1)}, f32[3,4096]{1,0:T(4,128)}, u32[]{:S(2)}) copy-start(f32[3,4096]{1,0:T(4,128)} %coords_ref.1) | copy-start | bytes 147460
  3.1 0.7 %copy-start.2 = (s32[16,256]{1,0:T(8,128)S(1)}, s32[16,256]{1,0:T(8,128)}, u32[]{:S(2)}) copy-start(s32[16,256]{1,0:T(8,128)} %order_ref.1) | copy-start | bytes 49156
